TPU v7x, 32 devices: a whole 2x2x4 slice. The times are simulated.
32 devices in a mesh: prow: 4 (over y, core), pcol: 8 (over z, x).
Axes of the slice: x: 2, y: 2, z: 4, core: 2. Of those that a mesh axis runs over, the one named last changes fastest.
Arguments:
- matrix: bfloat16 [2, 8, 4, 256, 2, 8, 256], P(None, None, 'prow', None, None, 'pcol'), may hold values from -6 to 6
Outputs:
- image: float32 [2, 8, 4, 256, 2, 8, 256], P(None, None, 'prow', None, None, 'pcol')
All inputs are finite; a program needn't handle non-finite values.
Results may differ from a plain program's by a relative error of at most 0.0003.
Values sent between devices are 32-bit elements; how exact they have to be, the bound alone decides.
A program may use at most 64 MiB of HBM per device.

v0:
```python
import jax
import jax.numpy as jnp
from jax import lax
from jax.sharding import PartitionSpec as P

HIGH = lax.Precision.HIGHEST


def prefix(value, axis, combine, identity):
    length, here = (lax.axis_size(axis), lax.axis_index(axis))
    everything = lax.all_gather(value, axis)
    start = jnp.broadcast_to(jnp.asarray(identity, value.dtype), value.shape)

    def lap(k, before):
        reached = k < here
        new = combine(before, everything[k])
        return jnp.where(reached, new, before)

    return lax.fori_loop(0, length, lap, start)


def add_terms(earlier, later):
    return earlier + later


def shards(matrix):
    batch = matrix.shape[0]
    rows_here = matrix.shape[1]
    tile_len = matrix.shape[3]
    cols_here = matrix.shape[4]
    prow_count = lax.axis_size("prow")
    pcol_count = lax.axis_size("pcol")
    prow_index = lax.axis_index("prow")
    pcol_index = lax.axis_index("pcol")
    local = matrix.astype(jnp.float32).reshape(batch, rows_here, tile_len, cols_here, tile_len)
    first_idx = lax.broadcasted_iota(jnp.int32, (tile_len, tile_len), 0)
    second_idx = lax.broadcasted_iota(jnp.int32, (tile_len, tile_len), 1)
    upper = (first_idx <= second_idx).astype(jnp.float32)
    lower = (second_idx <= first_idx).astype(jnp.float32)
    rowscan = jnp.einsum("nrick,kj->nricj", local, upper, precision=HIGH)
    row_sums = rowscan[:, :, :, :, tile_len - 1]
    gathered = lax.all_gather(row_sums, "pcol", axis=3, tiled=True)
    source = jnp.arange(pcol_count * cols_here, dtype=jnp.int32)
    source_glob = source % cols_here * pcol_count + source // cols_here
    target_glob = jnp.arange(cols_here, dtype=jnp.int32) * pcol_count + pcol_index
    earlier_mask = (source_glob[:, None] < target_glob[None, :]).astype(jnp.float32)
    row_carry = jnp.einsum("nrig,gc->nric", gathered, earlier_mask, precision=HIGH)
    rowscan = rowscan + row_carry[:, :, :, :, None]
    colscan = jnp.einsum("ik,nrkcj->nricj", lower, rowscan, precision=HIGH)
    col_sums = colscan[:, :, tile_len - 1, :, :]
    before = prefix(col_sums, "prow", add_terms, jnp.zeros_like(col_sums))
    whole = lax.psum(col_sums, "prow")
    strict = (jnp.arange(rows_here)[:, None] < jnp.arange(rows_here)[None, :]).astype(jnp.float32)
    col_carry = before + jnp.einsum("nscj,sr->nrcj", whole, strict, precision=HIGH)
    colscan = colscan + col_carry[:, :, None, :, :]
    row_glob = (
        jnp.arange(rows_here, dtype=jnp.int32)[:, None] * prow_count + prow_index
    ) * tile_len + jnp.arange(tile_len, dtype=jnp.int32)[None, :]
    col_glob = (
        jnp.arange(cols_here, dtype=jnp.int32)[:, None] * pcol_count + pcol_index
    ) * tile_len + jnp.arange(tile_len, dtype=jnp.int32)[None, :]
    row_factor = 1.0 / jnp.sqrt(row_glob.astype(jnp.float32) + 1.0)
    col_factor = 1.0 / jnp.sqrt(col_glob.astype(jnp.float32) + 1.0)
    scaled = colscan * (row_factor[None, :, :, None, None] * col_factor[None, None, None, :, :])
    return scaled.reshape(batch, rows_here, 1, tile_len, cols_here, 1, tile_len)


def solution(mesh):
    return jax.shard_map(
        shards,
        mesh=mesh,
        in_specs=(P(None, None, "prow", None, None, "pcol", None),),
        out_specs=P(None, None, "prow", None, None, "pcol", None),
        check_vma=False,
    )
```

profile of v0, /device:TPU:0, one launch (start us, length us, event | category | flops | bytes accessed | tf_op | source)
XLA Modules:
  0.0 76.3 jit_solution(13902189001919219110)
XLA Ops:
  0.0 3.5 %fusion.8 = f32[2,8,256,2,256]{2,4,3,1,0:T(8,128)S(1)} fusion(bf16[2,8,256,2,256]{4,3,2,1,0:T(2,128)(2,1)} %bitcast.44), kind=kOutput, calls=%fused_computation.10 | convolution fusion | flops 1073807360 | bytes 12582912 | tf_op jit(solution)/shard_map/nrick,kj->nricj/dot_general | solution.py:40
  3.5 28.3 %all-gather = f32[2,8,256,16,1]{2,4,3,1,0:T(1,128)S(1)} all-gather(f32[2,8,256,2,1]{2,4,3,1,0:T(1,128)S(1)} %slice.8), channel_id=2, replica_groups=mesh['prow'=4,'pcol'=8] {'pcol'}, dimensions={3}, use_global_device_ids=true | all-gather | bytes 294912 | tf_op jit(solution)/shard_map/all_gather | solution.py:42
  31.9 0.3 fusion.12
  32.2 4.9 %fusion.5 = f32[2,8,256,2,256]{4,2,3,1,0:T(8,128)S(1)} fusion(f32[2,8,256,2,256]{2,4,3,1,0:T(8,128)S(1)} %fusion.8, f32[2,8,256,2]{2,3,1,0:T(2,128)S(1)} %fusion.12), kind=kOutput, calls=%fused_computation.9 | convolution fusion | flops 6444613632 | bytes 16809984 | tf_op jit(solution)/shard_map/ik,nrkcj->nricj/dot_general | solution.py:49
  37.2 0.0 copy-start
  37.2 3.4 %copy-done = f32[2,8,256,2,256]{4,2,3,1,0:T(8,128)} copy-done((f32[2,8,256,2,256]{4,2,3,1,0:T(8,128)}, f32[2,8,256,2,256]{4,2,3,1,0:T(8,128)S(1)}, u32[]{:S(2)}) %copy-start) | copy-done | bytes 8388632
  40.6 5.4 %all-gather.1 = f32[8,8,1,2,256]{4,1,3,2,0:T(8,128)S(1)} all-gather(f32[2,8,1,2,256]{4,1,3,2,0:T(8,128)S(1)} %copy.10), channel_id=3, replica_groups=mesh['prow'=4,'pcol'=8] {'prow'}, dimensions={0}, use_global_device_ids=true | all-gather | bytes 163840 | tf_op jit(solution)/shard_map/all_gather | solution.py:11
  46.0 0.3 while.14
  46.3 11.6 %psum.7 = f32[2,8,2,256]{3,2,1,0:T(2,128)S(1)} all-reduce(f32[2,8,2,256]{3,2,1,0:T(2,128)S(1)} %bitcast.46), channel_id=1, replica_groups=mesh['prow'=4,'pcol'=8] {'prow'}, use_global_device_ids=true, to_apply=%region_2.3 | all-reduce | flops 8192 | bytes 65536 | tf_op jit(solution)/shard_map/psum | solution.py:52
  58.0 0.1 fusion.11
  58.1 0.1 add_rsqrt_fusion
  58.2 0.1 add_rsqrt_fusion.1
  58.3 2.3 %broadcast_multiply_fusion = f32[8,256,2,256]{3,1,2,0:T(8,128)} fusion(f32[2,256]{1,0:T(2,128)S(1)} %add_rsqrt_fusion.1, f32[8,256]{1,0:T(8,128)S(1)} %add_rsqrt_fusion), kind=kLoop, calls=%fused_computation.11 | loop fusion | flops 1048576 | bytes 4204544 | tf_op jit(solution)/shard_map/mul | solution.py:64
  60.6 5.8 %multiply_bitcast_fusion = f32[2,8,1,256,2,1,256]{6,3,4,1,0,5,2:T(8,128)S(1)} fusion(f32[2,8,256,2,256]{4,2,3,1,0:T(8,128)} %copy-done, f32[8,256,2,256]{3,1,2,0:T(8,128)} %broadcast_multiply_fusion, f32[2,8,2,256]{3,2,1,0:T(2,128)S(1)} %copy.14), kind=kLoop, calls=%fused_computation.3 | loop fusion | flops 4194304 | bytes 21004288 | tf_op jit(solution)/shard_map/reshape | solution.py:65
  66.4 9.9 %copy.15 = f32[2,8,1,256,2,1,256]{6,5,4,3,2,1,0:T(1,128)} copy(f32[2,8,1,256,2,1,256]{6,3,4,1,0,5,2:T(8,128)S(1)} %multiply_bitcast_fusion) | data formatting | bytes 16777216 | tf_op jit(solution)/shard_map/reshape | solution.py:65
  (18 shorter events, 0.3 us)
Async XLA Ops:
  37.2 3.4 %copy-start = (f32[2,8,256,2,256]{4,2,3,1,0:T(8,128)}, f32[2,8,256,2,256]{4,2,3,1,0:T(8,128)S(1)}, u32[]{:S(2)}) copy-start(f32[2,8,256,2,256]{4,2,3,1,0:T(8,128)S(1)} %fusion.5) | copy-start | bytes 25165828
where the time goes:
time: 76.5 us; the launch traced here: 76.3 us
  blocking collectives  45.4 us (59%)
  local copies, waits for them, and re-layouts  13.4 us (18%)
  matrix products  8.87 us (12%)
  other arithmetic  8.4 us (11%)
    all_gather x1, blocking collectives, shards(): gathered = lax.all_gather(row_sums, 'pcol', axis=3, tiled=True)  28.3 us
    psum x1, blocking collectives, shards(): whole = lax.psum(col_sums, 'prow')  11.6 us
    reshape x1, local copies, waits for them, and re-layouts, shards(): return scaled.reshape(batch, rows_here, 1, tile_len, cols_here, 1, tile_len)  9.91 us
    reshape x1, other arithmetic, shards(): return scaled.reshape(batch, rows_here, 1, tile_len, cols_here, 1, tile_len)  5.81 us
    all_gather x1, blocking collectives, prefix(): everything = lax.all_gather(value, axis)  5.42 us
    dot_general x1, matrix products, shards(): colscan = jnp.einsum('ik,nrkcj->nricj', lower, rowscan, precision=HIGH)  4.93 us
    dot_general x1, matrix products, shards(): rowscan = jnp.einsum('nrick,kj->nricj', local, upper, precision=HIGH)  3.48 us
    unnamed x3, local copies, waits for them, and re-layouts  3.41 us

commit v1 on v0

--- a/solution.py
+++ b/solution.py
@@ -49,7 +49,7 @@
     colscan = jnp.einsum("ik,nrkcj->nricj", lower, rowscan, precision=HIGH)
     col_sums = colscan[:, :, tile_len - 1, :, :]
     before = prefix(col_sums, "prow", add_terms, jnp.zeros_like(col_sums))
-    whole = lax.psum(col_sums, "prow")
+    whole = jnp.sum(lax.all_gather(col_sums, "prow"), axis=0)
     strict = (jnp.arange(rows_here)[:, None] < jnp.arange(rows_here)[None, :]).astype(jnp.float32)
     col_carry = before + jnp.einsum("nscj,sr->nrcj", whole, strict, precision=HIGH)
     colscan = colscan + col_carry[:, :, None, :, :]

time: 76.5 us -> 64.8 us (0.85)
  blocking collectives: 45.4 us -> 33.8 us
    psum x1 -> x0, blocking collectives: 11.6 us -> none  [shards(): whole = lax.psum(col_sums, 'prow')]
    unnamed x3 -> x2, local copies, waits for them, and re-layouts: 3.41 us -> 3.39 us
where the time goes in v1:
time: 64.8 us; the launch traced here: 64.7 us
  blocking collectives  33.8 us (52%)
  local copies, waits for them, and re-layouts  13.4 us (21%)
  matrix products  8.87 us (14%)
  other arithmetic  8.42 us (13%)
    all_gather x1, blocking collectives, shards(): gathered = lax.all_gather(row_sums, 'pcol', axis=3, tiled=True)  28.3 us
    reshape x1, local copies, waits for them, and re-layouts, shards(): return scaled.reshape(batch, rows_here, 1, tile_len, cols_here, 1, tile_len)  9.91 us
    reshape x1, other arithmetic, shards(): return scaled.reshape(batch, rows_here, 1, tile_len, cols_here, 1, tile_len)  5.81 us
    all_gather x1, blocking collectives, prefix(): everything = lax.all_gather(value, axis)  5.42 us
    dot_general x1, matrix products, shards(): colscan = jnp.einsum('ik,nrkcj->nricj', lower, rowscan, precision=HIGH)  4.93 us
    dot_general x1, matrix products, shards(): rowscan = jnp.einsum('nrick,kj->nricj', local, upper, precision=HIGH)  3.48 us
    unnamed x2, local copies, waits for them, and re-layouts  3.39 us
    mul x1, other arithmetic, shards(): row_factor[None, :, :, None, None] * col_factor[None, None, None, :, :]  2.27 us

profile of v1, /device:TPU:0, one launch (start us, length us, event | category | flops | bytes accessed | tf_op | source)
XLA Modules:
  0.0 64.7 jit_solution(12529521909542212022)
XLA Ops:
  0.0 3.5 %fusion.8 = f32[2,8,256,2,256]{2,4,3,1,0:T(8,128)S(1)} fusion(bf16[2,8,256,2,256]{4,3,2,1,0:T(2,128)(2,1)} %bitcast.42), kind=kOutput, calls=%fused_computation.10 | convolution fusion | flops 1073807360 | bytes 12582912 | tf_op jit(solution)/shard_map/nrick,kj->nricj/dot_general | solution.py:40
  3.5 28.3 %all-gather = f32[2,8,256,16,1]{2,4,3,1,0:T(1,128)S(1)} all-gather(f32[2,8,256,2,1]{2,4,3,1,0:T(1,128)S(1)} %slice.8), channel_id=2, replica_groups=mesh['prow'=4,'pcol'=8] {'pcol'}, dimensions={3}, use_global_device_ids=true | all-gather | bytes 294912 | tf_op jit(solution)/shard_map/all_gather | solution.py:42
  31.9 0.3 fusion.12
  32.2 4.9 %fusion.5 = f32[2,8,256,2,256]{4,2,3,1,0:T(8,128)S(1)} fusion(f32[2,8,256,2,256]{2,4,3,1,0:T(8,128)S(1)} %fusion.8, f32[2,8,256,2]{2,3,1,0:T(2,128)S(1)} %fusion.12), kind=kOutput, calls=%fused_computation.9 | convolution fusion | flops 6444613632 | bytes 16809984 | tf_op jit(solution)/shard_map/ik,nrkcj->nricj/dot_general | solution.py:49
  37.2 0.0 copy-start
  37.2 3.4 %copy-done = f32[2,8,256,2,256]{4,2,3,1,0:T(8,128)} copy-done((f32[2,8,256,2,256]{4,2,3,1,0:T(8,128)}, f32[2,8,256,2,256]{4,2,3,1,0:T(8,128)S(1)}, u32[]{:S(2)}) %copy-start) | copy-done | bytes 8388632
  40.6 5.4 %all-gather.1 = f32[8,8,1,2,256]{4,1,3,2,0:T(8,128)S(1)} all-gather(f32[2,8,1,2,256]{4,1,3,2,0:T(8,128)S(1)} %copy.9), channel_id=3, replica_groups=mesh['prow'=4,'pcol'=8] {'prow'}, dimensions={0}, use_global_device_ids=true | all-gather | bytes 163840 | tf_op jit(solution)/shard_map/all_gather | solution.py:11
  46.0 0.3 while.14
  46.3 0.1 fusion.11
  46.5 0.1 add_rsqrt_fusion
  46.6 0.1 add_rsqrt_fusion.1
  46.7 2.3 %broadcast_multiply_fusion = f32[8,256,2,256]{3,1,2,0:T(8,128)} fusion(f32[2,256]{1,0:T(2,128)S(1)} %add_rsqrt_fusion.1, f32[8,256]{1,0:T(8,128)S(1)} %add_rsqrt_fusion), kind=kLoop, calls=%fused_computation.11 | loop fusion | flops 1048576 | bytes 4204544 | tf_op jit(solution)/shard_map/mul | solution.py:64
  48.9 5.8 %multiply_bitcast_fusion = f32[2,8,1,256,2,1,256]{6,3,4,1,0,5,2:T(8,128)S(1)} fusion(f32[2,8,256,2,256]{4,2,3,1,0:T(8,128)} %copy-done, f32[8,256,2,256]{3,1,2,0:T(8,128)} %broadcast_multiply_fusion, f32[2,8,2,256]{3,2,1,0:T(2,128)S(1)} %copy.14), kind=kLoop, calls=%fused_computation.3 | loop fusion | flops 4194304 | bytes 21004288 | tf_op jit(solution)/shard_map/reshape | solution.py:65
  54.8 9.9 %copy.15 = f32[2,8,1,256,2,1,256]{6,5,4,3,2,1,0:T(1,128)} copy(f32[2,8,1,256,2,1,256]{6,3,4,1,0,5,2:T(8,128)S(1)} %multiply_bitcast_fusion) | data formatting | bytes 16777216 | tf_op jit(solution)/shard_map/reshape | solution.py:65
  (18 shorter events, 0.3 us)
Async XLA Ops:
  37.2 3.4 %copy-start = (f32[2,8,256,2,256]{4,2,3,1,0:T(8,128)}, f32[2,8,256,2,256]{4,2,3,1,0:T(8,128)S(1)}, u32[]{:S(2)}) copy-start(f32[2,8,256,2,256]{4,2,3,1,0:T(8,128)S(1)} %fusion.5) | copy-start | bytes 25165828
